TPU v7x, 32 devices: a whole 2x2x4 slice. The times are simulated.
32 devices in a mesh: types: 16 (over z, y, x), tm: 2 (over core).
Axes of the slice: x: 2, y: 2, z: 4, core: 2. Of those that a mesh axis runs over, the one named last changes fastest.
Arguments:
- brackets: int32 [96, 8, 7, 512], P('types', 'tm'), may hold values from 0 to 510, as said below
- active_blocks: int32 [96], P('types'), may hold values from 1 to 4, as said below
- initial_mass: float32 [96, 7, 512], P('types'), may hold values from 0 to 0.00055803574
- patience: float32 [96], P('types'), may hold values from 0.9 to 0.985
- productivity: float32 [96], P('types'), may hold values from 0.5 to 2
- income_levels: float32 [7], replicated, may hold values from 0.3 to 3
- income_transition: float32 [7, 7], replicated, may hold values from 0 to 1, as said below
- wage_path: float32 [8], replicated, may hold values from 0.8 to 1.2
- bond_supply: float32 [8], replicated, may hold values from 0.5 to 2
- price_guess: float32 [8], replicated, may hold values from -3 to 3
- jac_inverse: float32 [8, 8], replicated, may hold values from -2 to 2
- assignment: int32 [96], replicated, may hold values from 0 to 95, each once
Outputs:
- price_path: float32 [8], replicated
- market_gap: float32 [8], replicated
- type_paths: float32 [96, 2, 8], P('types')
Inputs may be any that keep to these rules, and one draw needn't show every extreme that they name: `brackets`: the bracket of asset point i lies between max(i - 9, 0) and max(i - 1, 0). `active_blocks`: counts of 128-point blocks from the bottom of the grid. `income_transition`: rows of positive entries summing to one. `assignment`: each type appears once.
All inputs are finite; a program needn't handle non-finite values.
Results may differ from a plain program's by a relative error of at most 0.0003.
Values sent between devices are 32-bit elements; how exact they have to be, the bound alone decides.
A program may use at most 64 MiB of HBM per device.

v0:
```python
import jax
import jax.numpy as jnp
from jax import lax
from jax.sharding import PartitionSpec as P

ASSETS = 512
BLOCK = 128
NEWTON = 2
grid_top = 40.0
rate_floor = 0.005
rate_span = 0.03
highest = lax.Precision.HIGHEST


def asset_grid(points):
    return grid_top * (points / (ASSETS - 1)) ** 2


def interest(price_path):
    return rate_floor + rate_span * jax.nn.sigmoid(price_path)


def policy(lower_edge, upper_edge, bracket_now, rate_now, income_now, grid_rows):
    grid_low = asset_grid(bracket_now.astype(jnp.float32))
    grid_high = asset_grid((bracket_now + 1).astype(jnp.float32))
    spacing = jnp.maximum(upper_edge - lower_edge, (grid_high - grid_low) / (1.0 + rate_now))
    weight_up = jnp.clip((grid_rows[None, :] - lower_edge) / spacing, 0.0, 1.0)
    savings = grid_low + weight_up * (grid_high - grid_low)
    spending = (1.0 + rate_now) * grid_rows[None, :] + income_now[:, None] - savings
    return (weight_up, savings, spending)


def band_table(bracket_rows, window):
    targets = window + jnp.arange(2 * BLOCK, dtype=jnp.int32)
    return (bracket_rows[:, :, None] == targets[None, None, :]).astype(jnp.float32)


def backward_type(bracket, blocks, patience, incomes, interest_path, values_end, transition):
    grid_values = asset_grid(jnp.arange(ASSETS, dtype=jnp.float32))
    income_count = values_end.shape[0]

    def backward_period(values, inputs):
        bracket_now, rate_now, income_now = inputs
        expected = patience * jnp.dot(transition, values, precision=highest)
        endogenous = (1.0 / expected + grid_values[None, :] - income_now[:, None]) / (
            1.0 + rate_now
        )
        following = jnp.concatenate([endogenous[:, 1:], endogenous[:, -1:]], axis=1)
        stacked = jnp.stack([endogenous, following])

        def backward_block_rows(block_index, carried):
            row_start = block_index * BLOCK
            window = jnp.maximum(row_start - BLOCK, 0)
            bracket_rows = lax.dynamic_slice_in_dim(bracket_now, row_start, BLOCK, 1)
            onehot = band_table(bracket_rows, window)
            stacked_window = lax.dynamic_slice_in_dim(stacked, window, 2 * BLOCK, 2)
            picked = jnp.einsum("eia,cea->cei", onehot, stacked_window, precision=highest)
            grid_rows = lax.dynamic_slice_in_dim(grid_values, row_start, BLOCK, 0)
            weight_up, savings, spending = policy(
                picked[0], picked[1], bracket_rows, rate_now, income_now, grid_rows
            )
            fresh = (weight_up, savings, spending, (1.0 + rate_now) / spending)
            return tuple(
                (
                    lax.dynamic_update_slice_in_dim(target_array, piece_array, row_start, 1)
                    for target_array, piece_array in zip(carried, fresh)
                )
            )

        zeros_rows = jnp.zeros((income_count, ASSETS), jnp.float32)
        ones_rows = jnp.ones((income_count, ASSETS), jnp.float32)
        weight_up, savings, spending, values_new = lax.fori_loop(
            0, blocks, backward_block_rows, (zeros_rows, zeros_rows, ones_rows, ones_rows)
        )
        return (values_new, (weight_up, savings, spending))

    return lax.scan(backward_period, values_end, (bracket, interest_path, incomes), reverse=True)


def forward_type(bracket, blocks, weight_up, savings, spending, mass_start, transition):

    def forward_period(masses, inputs):
        bracket_now, weight_now, savings_now, spending_now = inputs
        totals = jnp.stack([jnp.sum(masses * savings_now), jnp.sum(masses * spending_now)])
        weights = jnp.stack([(1.0 - weight_now) * masses, weight_now * masses])

        def forward_block_rows(block_index, shifted_mass):
            row_start = block_index * BLOCK
            window = jnp.maximum(row_start - BLOCK, 0)
            bracket_rows = lax.dynamic_slice_in_dim(bracket_now, row_start, BLOCK, 1)
            onehot = band_table(bracket_rows, window)
            weight_rows = lax.dynamic_slice_in_dim(weights, row_start, BLOCK, 2)
            contrib = jnp.einsum("eia,cei->cea", onehot, weight_rows, precision=highest)
            current = lax.dynamic_slice_in_dim(shifted_mass, window, 2 * BLOCK, 2)
            return lax.dynamic_update_slice_in_dim(shifted_mass, current + contrib, window, 2)

        shifted_mass = lax.fori_loop(0, blocks, forward_block_rows, jnp.zeros_like(weights))
        arrived = shifted_mass[0] + jnp.concatenate(
            [jnp.zeros_like(shifted_mass[1][:, :1]), shifted_mass[1][:, :-1]], axis=1
        )
        return (jnp.dot(transition.T, arrived, precision=highest), totals)

    masses_end, type_series = lax.scan(
        forward_period, mass_start, (bracket, weight_up, savings, spending)
    )
    return (masses_end, type_series.T)


def body(
    brackets,
    active_blocks,
    initial_mass,
    patience,
    productivity,
    income_levels,
    income_transition,
    wage_path,
    bond_supply,
    price_guess,
    jac_inverse,
    assignment,
):
    local_types = patience.shape[0]
    all_types = local_types * lax.axis_size("types")
    core_count = lax.axis_size("tm")
    core_index = lax.axis_index("tm")
    columns = jnp.arange(ASSETS, dtype=jnp.int32)
    grid_values = asset_grid(columns.astype(jnp.float32))
    type_numbers = (
        lax.axis_index("types") * local_types + jnp.arange(local_types, dtype=jnp.int32)
    ).astype(jnp.float32)
    half_types = local_types // core_count
    brackets_mine = lax.all_to_all(brackets, "tm", split_axis=0, concat_axis=1, tiled=True)

    def take_mine(target_array):
        return lax.dynamic_slice_in_dim(target_array, core_index * half_types, half_types, 0)

    blocks_mine = take_mine(active_blocks)
    patience_mine = take_mine(patience)
    productivity_mine = take_mine(productivity)
    mass_mine = take_mine(initial_mass)
    numbers_mine = take_mine(type_numbers)
    live_rows = (columns[None, None, :] < blocks_mine[:, None, None] * BLOCK).astype(jnp.float32)
    mass_start = mass_mine * live_rows
    price_path = price_guess
    market_gap = jnp.zeros_like(price_guess)
    everything = None
    for newton_round in range(NEWTON):
        interest_path = interest(price_path)
        last_rate = interest_path[-1]
        ends_income = wage_path[-1] * productivity_mine[:, None] * income_levels[None, :]
        values_end = (1.0 + last_rate) / (
            last_rate * grid_values[None, None, :] + ends_income[:, :, None]
        )
        interest_here = interest_path
        incomes = (
            wage_path[None, :, None]
            * productivity_mine[:, None, None]
            * income_levels[None, None, :]
        )

        def sweep_solve_member(members):
            return backward_type(
                members[0],
                members[1],
                members[2],
                members[3],
                interest_here,
                members[4],
                income_transition,
            )

        values_start, solve_policies = lax.map(
            sweep_solve_member, (brackets_mine, blocks_mine, patience_mine, incomes, values_end)
        )

        def solve_member(members):
            return forward_type(
                members[0],
                members[1],
                members[2],
                members[3],
                members[4],
                members[5],
                income_transition,
            )

        masses_end, solve_type_series = lax.map(
            solve_member,
            (
                brackets_mine,
                blocks_mine,
                solve_policies[0],
                solve_policies[1],
                solve_policies[2],
                mass_start,
            ),
        )
        local_sum = jnp.sum(solve_type_series[:, 0, :], axis=0)
        totals = lax.psum(local_sum, ("types", "tm"))
        if newton_round + 1 == NEWTON:
            everything = (
                lax.all_gather(solve_type_series, ("types", "tm"), axis=0, tiled=True),
                lax.all_gather(numbers_mine, ("types", "tm"), axis=0, tiled=True),
            )
        market_gap = totals / all_types - bond_supply
        price_path = price_path - jnp.dot(jac_inverse, market_gap, precision=highest)
    slot_types = lax.dynamic_slice_in_dim(
        assignment, lax.axis_index("types") * local_types, local_types, 0
    ).astype(jnp.float32)
    select = (slot_types[:, None] == everything[1][None, :]).astype(jnp.float32)
    type_paths = jnp.einsum("st,tcp->scp", select, everything[0], precision=highest)
    return (price_path, market_gap, type_paths)


def solution(mesh):
    placed = (
        P("types", "tm", None, None),
        P("types"),
        P("types", None, None),
        P("types"),
        P("types"),
        P(),
        P(),
        P(),
        P(),
        P(),
        P(),
        P(),
    )
    return jax.shard_map(
        body,
        mesh=mesh,
        in_specs=placed,
        out_specs=(P(), P(), P("types", None, None)),
        check_vma=False,
    )
```

profile of v0, /device:TPU:14, one launch (start us, length us, event | category | flops | bytes accessed | tf_op | source)
XLA Modules:
  0.0 985.2 jit_solution(13439941722664523661)
XLA Ops:
  12.0 147.5 %while.321 = (s32[]{:T(128)}, f32[3,8,7,512]{3,2,1,0:T(8,128)S(1)}, f32[3,8,7,512]{3,2,1,0:T(8,128)S(1)}, f32[3,8,7,512]{3,2,1,0:T(8,128)S(1)}, f32[3,7,512]{2,1...) while((s32[]{:T(128)}, f32[3,8,7,512]{3,2,1,0:T(8,128)S(1)}, ...), condition=%wide.region_5.6_spmd, body=%wide.region_0.5_spmd.sunk | while | flops 6097422 | bytes 1872705 | solution.py:173
  13.4 47.7 %while.328 = (s32[]{:T(128)}, f32[7,512]{1,0:T(8,128)S(1)}, f32[8,7,512]{2,1,0:T(8,128)S(1)}, f32[8,7,512]{2,1,0:T(8,128)S(1)}, f32[8,7,512]{2,1,0:T(8,128)S(1)}...) while((s32[]{:T(128)}, f32[7,512]{1,0:T(8,128)S(1)}, ...), condition=%wide.region_4.4_spmd.clone.clone, body=%wide.region_1.3_spmd.clone.clone.sunk | while | flops 6097420 | bytes 483244 | solution.py:77
  21.7 3.6 while.335
  27.7 3.6 while.335
  62.6 47.7 %while.328 = (s32[]{:T(128)}, f32[7,512]{1,0:T(8,128)S(1)}, f32[8,7,512]{2,1,0:T(8,128)S(1)}, f32[8,7,512]{2,1,0:T(8,128)S(1)}, f32[8,7,512]{2,1,0:T(8,128)S(1)}...) while((s32[]{:T(128)}, f32[7,512]{1,0:T(8,128)S(1)}, ...), condition=%wide.region_4.4_spmd.clone.clone, body=%wide.region_1.3_spmd.clone.clone.sunk | while | flops 6097420 | bytes 483244 | solution.py:77
  70.9 3.6 while.335
  76.8 3.6 while.335
  106.7 3.6 while.335
  111.8 47.7 %while.328 = (s32[]{:T(128)}, f32[7,512]{1,0:T(8,128)S(1)}, f32[8,7,512]{2,1,0:T(8,128)S(1)}, f32[8,7,512]{2,1,0:T(8,128)S(1)}, f32[8,7,512]{2,1,0:T(8,128)S(1)}...) while((s32[]{:T(128)}, f32[7,512]{1,0:T(8,128)S(1)}, ...), condition=%wide.region_4.4_spmd.clone.clone, body=%wide.region_1.3_spmd.clone.clone.sunk | while | flops 6097420 | bytes 483244 | solution.py:77
  114.1 3.6 while.335
  120.1 3.6 while.335
  149.9 3.6 while.335
  155.9 3.6 while.335
  159.7 143.2 %while.323 = (s32[]{:T(128)}, f32[3,2,8]{2,1,0:T(2,128)S(1)}, f32[3,7,512]{2,1,0:T(8,128)S(1)}, s32[3,8,7,512]{3,2,1,0:T(8,128)S(1)}, f32[3,8,7,512]{3,2,1,0:T(8...) while((s32[]{:T(128)}, f32[3,2,8]{2,1,0:T(2,128)S(1)}, ...), condition=%wide.region_13.14_spmd, body=%wide.region_6.13_spmd.sunk | while | flops 6075148 | bytes 1450953 | solution.py:188
  160.4 46.9 %while.329 = (s32[]{:T(128)}, f32[7,512]{1,0:T(8,128)S(1)}, f32[8,2]{1,0:T(8,128)S(1)}, s32[8,7,512]{2,1,0:T(8,128)S(1)}, f32[8,7,512]{2,1,0:T(8,128)S(1)}, /*in...) while((s32[]{:T(128)}, f32[7,512]{1,0:T(8,128)S(1)}, ...), condition=%wide.region_12.12_spmd, body=%wide.region_7.11_spmd.sunk | while | flops 6075146 | bytes 502252 | solution.py:103
  208.1 46.9 %while.329 = (s32[]{:T(128)}, f32[7,512]{1,0:T(8,128)S(1)}, f32[8,2]{1,0:T(8,128)S(1)}, s32[8,7,512]{2,1,0:T(8,128)S(1)}, f32[8,7,512]{2,1,0:T(8,128)S(1)}, /*in...) while((s32[]{:T(128)}, f32[7,512]{1,0:T(8,128)S(1)}, ...), condition=%wide.region_12.12_spmd, body=%wide.region_7.11_spmd.sunk | while | flops 6075146 | bytes 502252 | solution.py:103
  255.8 46.9 %while.329 = (s32[]{:T(128)}, f32[7,512]{1,0:T(8,128)S(1)}, f32[8,2]{1,0:T(8,128)S(1)}, s32[8,7,512]{2,1,0:T(8,128)S(1)}, f32[8,7,512]{2,1,0:T(8,128)S(1)}, /*in...) while((s32[]{:T(128)}, f32[7,512]{1,0:T(8,128)S(1)}, ...), condition=%wide.region_12.12_spmd, body=%wide.region_7.11_spmd.sunk | while | flops 6075146 | bytes 502252 | solution.py:103
  302.9 174.0 %psum.14 = f32[8]{0:T(128)S(1)} all-reduce(f32[8]{0:T(128)S(1)} %slice_reduce_fusion.1), channel_id=1, replica_groups=mesh['types'=16,'tm'=2] {'types','tm'}, use_global_device_ids=true, to_apply=%region_15.16 | all-reduce | flops 8 | bytes 64 | tf_op jit(solution)/shard_map/psum | solution.py:200
  479.2 147.6 %while.325 = (s32[]{:T(128)}, f32[3,8,7,512]{3,2,1,0:T(8,128)S(1)}, f32[3,8,7,512]{3,2,1,0:T(8,128)S(1)}, f32[3,8,7,512]{3,2,1,0:T(8,128)S(1)}, f32[3,7,512]{2,1...) while((s32[]{:T(128)}, f32[3,8,7,512]{3,2,1,0:T(8,128)S(1)}, ...), condition=%wide.region_21.22_spmd, body=%wide.region_16.21_spmd.sunk | while | flops 6097422 | bytes 1872697 | solution.py:173
  480.6 47.7 %while.330 = (s32[]{:T(128)}, f32[7,512]{1,0:T(8,128)S(1)}, f32[8,7,512]{2,1,0:T(8,128)S(1)}, f32[8,7,512]{2,1,0:T(8,128)S(1)}, f32[8,7,512]{2,1,0:T(8,128)S(1)}...) while((s32[]{:T(128)}, f32[7,512]{1,0:T(8,128)S(1)}, ...), condition=%wide.region_20.20_spmd.clone.clone, body=%wide.region_17.19_spmd.clone.clone.sunk | while | flops 6097420 | bytes 483244 | solution.py:77
  482.9 3.6 while.333
  518.7 3.6 while.333
  524.6 3.6 while.333
  529.8 47.7 %while.330 = (s32[]{:T(128)}, f32[7,512]{1,0:T(8,128)S(1)}, f32[8,7,512]{2,1,0:T(8,128)S(1)}, f32[8,7,512]{2,1,0:T(8,128)S(1)}, f32[8,7,512]{2,1,0:T(8,128)S(1)}...) while((s32[]{:T(128)}, f32[7,512]{1,0:T(8,128)S(1)}, ...), condition=%wide.region_20.20_spmd.clone.clone, body=%wide.region_17.19_spmd.clone.clone.sunk | while | flops 6097420 | bytes 483244 | solution.py:77
  538.0 3.6 while.333
  578.9 47.7 %while.330 = (s32[]{:T(128)}, f32[7,512]{1,0:T(8,128)S(1)}, f32[8,7,512]{2,1,0:T(8,128)S(1)}, f32[8,7,512]{2,1,0:T(8,128)S(1)}, f32[8,7,512]{2,1,0:T(8,128)S(1)}...) while((s32[]{:T(128)}, f32[7,512]{1,0:T(8,128)S(1)}, ...), condition=%wide.region_20.20_spmd.clone.clone, body=%wide.region_17.19_spmd.clone.clone.sunk | while | flops 6097420 | bytes 483244 | solution.py:77
  626.8 143.2 %while.327 = (s32[]{:T(128)}, f32[3,2,8]{2,1,0:T(2,128)S(1)}, f32[3,7,512]{2,1,0:T(8,128)S(1)}, s32[3,8,7,512]{3,2,1,0:T(8,128)S(1)}, f32[3,8,7,512]{3,2,1,0:T(8...) while((s32[]{:T(128)}, f32[3,2,8]{2,1,0:T(2,128)S(1)}, ...), condition=%wide.region_29.30_spmd, body=%wide.region_22.29_spmd.sunk | while | flops 6075148 | bytes 1450953 | solution.py:188
  627.5 46.9 %while.331 = (s32[]{:T(128)}, f32[7,512]{1,0:T(8,128)S(1)}, f32[8,2]{1,0:T(8,128)S(1)}, s32[8,7,512]{2,1,0:T(8,128)S(1)}, f32[8,7,512]{2,1,0:T(8,128)S(1)}, /*in...) while((s32[]{:T(128)}, f32[7,512]{1,0:T(8,128)S(1)}, ...), condition=%wide.region_28.28_spmd, body=%wide.region_23.27_spmd.sunk | while | flops 6075146 | bytes 502252 | solution.py:103
  675.2 46.9 %while.331 = (s32[]{:T(128)}, f32[7,512]{1,0:T(8,128)S(1)}, f32[8,2]{1,0:T(8,128)S(1)}, s32[8,7,512]{2,1,0:T(8,128)S(1)}, f32[8,7,512]{2,1,0:T(8,128)S(1)}, /*in...) while((s32[]{:T(128)}, f32[7,512]{1,0:T(8,128)S(1)}, ...), condition=%wide.region_28.28_spmd, body=%wide.region_23.27_spmd.sunk | while | flops 6075146 | bytes 502252 | solution.py:103
  722.9 46.9 %while.331 = (s32[]{:T(128)}, f32[7,512]{1,0:T(8,128)S(1)}, f32[8,2]{1,0:T(8,128)S(1)}, s32[8,7,512]{2,1,0:T(8,128)S(1)}, f32[8,7,512]{2,1,0:T(8,128)S(1)}, /*in...) while((s32[]{:T(128)}, f32[7,512]{1,0:T(8,128)S(1)}, ...), condition=%wide.region_28.28_spmd, body=%wide.region_23.27_spmd.sunk | while | flops 6075146 | bytes 502252 | solution.py:103
  770.0 166.2 %all_gather.7 = f32[96,2,8]{2,1,0:T(2,128)S(1)} all-gather(f32[3,2,8]{2,1,0:T(2,128)S(1)} %get-tuple-element.1994), channel_id=1, replica_groups=mesh['types'=16,'tm'=2] {'types','tm'}, dimensions={0}, use_global_device_ids=true | all-gather | bytes 6336 | tf_op jit(solution)/shard_map/all_gather | solution.py:203
  936.2 46.3 %all-reduce.3 = (f32[8]{0:T(128)S(1)}, f32[96]{0:T(128)S(1)}) all-reduce(f32[8]{0:T(128)S(1)} %slice_reduce_fusion, f32[96]{0:T(128)S(1)} %get-tuple-element.2439), channel_id=1, replica_groups=mesh['types'=16,'tm'=2] {'types','tm'}, use_global_device_ids=true, to_apply=%region_31.32 | all-reduce | flops 104 | bytes 832 | tf_op jit(solution)/shard_map/psum | solution.py:200
  (2652 shorter events, 654.6 us)
Async XLA Ops:
  0.6 476.3 %copy-start = (f32[8,8]{1,0:T(8,128)S(1)}, f32[8,8]{1,0:T(8,128)}, u32[]{:S(2)}) copy-start(f32[8,8]{1,0:T(8,128)} %param.46) | copy-start | bytes 772
  0.6 10.4 %all-to-all-start = ((s32[6,4,7,512]{3,1,2,0:T(4,128)}), s32[6,4,7,512]{3,1,2,0:T(4,128)S(1)}, u32[]{:S(2)}, u32[]{:S(2)}) async-start(s32[6,4,7,512]{3,1,2,0:T(4,128)} %param.36), calls=%async_computation | async-start | bytes 688128 | tf_op jit(solution)/shard_map/all_to_all | solution.py:133
  4.1 0.7 copy-start.3
  4.8 0.7 copy-start.8
  7.4 0.7 copy-start.5
  8.9 0.7 copy-start.2
  9.6 0.7 copy-start.4
  10.3 0.7 copy-start.7
  11.3 0.7 copy-start.6
  12.0 147.6 %copy-start.1 = (f32[6,7,512]{2,1,0:T(8,128)S(1)}, f32[6,7,512]{2,1,0:T(8,128)}, u32[]{:S(2)}) copy-start(f32[6,7,512]{2,1,0:T(8,128)} %param.38) | copy-start | bytes 258052
  302.9 174.0 %copy-start.10 = (f32[8]{0:T(128)S(1)}, f32[8]{0:T(128)}, u32[]{:S(2)}) copy-start(f32[8]{0:T(128)} %param.44) | copy-start | bytes 100
  982.5 0.7 copy-start.9
  984.1 0.5 copy-start.11
where the time goes:
time: 992 us; the launch traced here: 985 us
  blocking collectives  387 us (39%)
  loops' own time  232 us (23%)
  matrix products  142 us (14%)
  other arithmetic  126 us (13%)
  local copies, waits for them, and re-layouts  92.5 us (9%)
    psum x2, blocking collectives, body(): totals = lax.psum(local_sum, ('types', 'tm'))  220 us
    all_gather x1, blocking collectives, body(): lax.all_gather(solve_type_series, ('types', 'tm'), axis=0, tiled=True)  166 us
    another operation x48, loops' own time, forward_period(): lax.fori_loop(0, blocks, forward_block_rows, jnp.zeros_like(weights))  98.9 us
    another operation x48, loops' own time, backward_period(): lax.fori_loop(0, blocks, backward_block_rows, (zeros_rows, zeros_rows, on...  95.8 us
    broadcast_in_dim x48, other arithmetic, forward_type(): lax.scan(forward_period, mass_start, (bracket, weight_up, savings, spendi...  64.1 us
    dot_general x96, matrix products, backward_block_rows(): jnp.einsum('eia,cea->cei', onehot, stacked_window, precision=highest)  53.3 us
    dot_general x96, matrix products, forward_block_rows(): contrib = jnp.einsum('eia,cei->cea', onehot, weight_rows, precision=highest)  39.9 us
    dot_general x48, matrix products, backward_period(): expected = patience * jnp.dot(transition, values, precision=highest)  37.1 us
  transfers between devices with their start and end apart: 1, of which 0 were waited for; matrix products, arithmetic and copies ran while one was open for 0% of the time, Pallas kernels for 0%

commit v1 on v0

--- a/solution.py
+++ b/solution.py
@@ -197,7 +197,7 @@
             ),
         )
         local_sum = jnp.sum(solve_type_series[:, 0, :], axis=0)
-        totals = lax.psum(local_sum, ("types", "tm"))
+        totals = lax.psum(lax.psum(local_sum, "tm"), "types")
         if newton_round + 1 == NEWTON:
             everything = (
                 lax.all_gather(solve_type_series, ("types", "tm"), axis=0, tiled=True),

time: 992 us -> 1020 us (1.028); the launches traced: 985 us -> 997 us
  blocking collectives: 387 us -> 408 us
    unnamed x0 -> x1, blocking collectives: none -> 46.2 us
    psum x2 -> x4, blocking collectives: 220 us -> 196 us  [body(): totals = lax.psum(lax.psum(local_sum, 'tm'), 'types')]
where the time goes in v1:
time: 1020 us; the launch traced here: 997 us
  blocking collectives  408 us (40%)
  loops' own time  226 us (22%)
  matrix products  142 us (14%)
  other arithmetic  121 us (12%)
  local copies, waits for them, and re-layouts  93.3 us (9%)
    psum x4, blocking collectives, body(): totals = lax.psum(lax.psum(local_sum, 'tm'), 'types')  196 us
    all_gather x1, blocking collectives, body(): lax.all_gather(solve_type_series, ('types', 'tm'), axis=0, tiled=True)  165 us
    another operation x48, loops' own time, forward_period(): lax.fori_loop(0, blocks, forward_block_rows, jnp.zeros_like(weights))  98.9 us
    another operation x48, loops' own time, backward_period(): lax.fori_loop(0, blocks, backward_block_rows, (zeros_rows, zeros_rows, on...  87 us
    broadcast_in_dim x48, other arithmetic, forward_type(): lax.scan(forward_period, mass_start, (bracket, weight_up, savings, spendi...  61.4 us
    dot_general x96, matrix products, backward_block_rows(): jnp.einsum('eia,cea->cei', onehot, stacked_window, precision=highest)  53.3 us
    unnamed x1, blocking collectives  46.2 us
    dot_general x96, matrix products, forward_block_rows(): contrib = jnp.einsum('eia,cei->cea', onehot, weight_rows, precision=highest)  39.9 us
  transfers between devices with their start and end apart: 1, of which 0 were waited for; matrix products, arithmetic and copies ran while one was open for 0% of the time, Pallas kernels for 0%

profile of v1, /device:TPU:14, one launch (start us, length us, event | category | flops | bytes accessed | tf_op | source)
XLA Modules:
  0.0 997.1 jit_solution(14698498611541894410)
XLA Ops:
  0.6 3.5 all-to-all-start
  12.0 145.1 %while.321 = (s32[]{:T(128)}, f32[3,8,7,512]{3,2,1,0:T(8,128)S(1)}, f32[3,8,7,512]{3,2,1,0:T(8,128)S(1)}, f32[3,8,7,512]{3,2,1,0:T(8,128)S(1)}, f32[3,7,512]{2,1...) while((s32[]{:T(128)}, f32[3,8,7,512]{3,2,1,0:T(8,128)S(1)}, ...), condition=%wide.region_5.6_spmd, body=%wide.region_0.5_spmd.sunk | while | flops 6097422 | bytes 1872705 | solution.py:173
  13.3 47.0 %while.328 = (s32[]{:T(128)}, f32[7,512]{1,0:T(8,128)S(1)}, f32[8,7,512]{2,1,0:T(8,128)S(1)}, f32[8,7,512]{2,1,0:T(8,128)S(1)}, f32[8,7,512]{2,1,0:T(8,128)S(1)}...) while((s32[]{:T(128)}, f32[7,512]{1,0:T(8,128)S(1)}, ...), condition=%wide.region_4.4_spmd.clone.clone, body=%wide.region_1.3_spmd.clone.clone.sunk | while | flops 6097420 | bytes 483244 | solution.py:77
  61.7 47.0 %while.328 = (s32[]{:T(128)}, f32[7,512]{1,0:T(8,128)S(1)}, f32[8,7,512]{2,1,0:T(8,128)S(1)}, f32[8,7,512]{2,1,0:T(8,128)S(1)}, f32[8,7,512]{2,1,0:T(8,128)S(1)}...) while((s32[]{:T(128)}, f32[7,512]{1,0:T(8,128)S(1)}, ...), condition=%wide.region_4.4_spmd.clone.clone, body=%wide.region_1.3_spmd.clone.clone.sunk | while | flops 6097420 | bytes 483244 | solution.py:77
  110.0 47.0 %while.328 = (s32[]{:T(128)}, f32[7,512]{1,0:T(8,128)S(1)}, f32[8,7,512]{2,1,0:T(8,128)S(1)}, f32[8,7,512]{2,1,0:T(8,128)S(1)}, f32[8,7,512]{2,1,0:T(8,128)S(1)}...) while((s32[]{:T(128)}, f32[7,512]{1,0:T(8,128)S(1)}, ...), condition=%wide.region_4.4_spmd.clone.clone, body=%wide.region_1.3_spmd.clone.clone.sunk | while | flops 6097420 | bytes 483244 | solution.py:77
  157.2 140.8 %while.323 = (s32[]{:T(128)}, f32[3,2,8]{2,1,0:T(2,128)S(1)}, f32[3,7,512]{2,1,0:T(8,128)S(1)}, s32[3,8,7,512]{3,2,1,0:T(8,128)S(1)}, f32[3,8,7,512]{3,2,1,0:T(8...) while((s32[]{:T(128)}, f32[3,2,8]{2,1,0:T(2,128)S(1)}, ...), condition=%wide.region_13.14_spmd, body=%wide.region_6.13_spmd.sunk | while | flops 6075148 | bytes 1450953 | solution.py:188
  157.9 46.2 %while.329 = (s32[]{:T(128)}, f32[7,512]{1,0:T(8,128)S(1)}, f32[8,2]{1,0:T(8,128)S(1)}, s32[8,7,512]{2,1,0:T(8,128)S(1)}, f32[8,7,512]{2,1,0:T(8,128)S(1)}, /*in...) while((s32[]{:T(128)}, f32[7,512]{1,0:T(8,128)S(1)}, ...), condition=%wide.region_12.12_spmd, body=%wide.region_7.11_spmd.sunk | while | flops 6075146 | bytes 502252 | solution.py:103
  158.6 3.4 while.334
  164.4 3.4 while.334
  170.2 3.4 while.334
  176.0 3.4 while.334
  181.7 3.4 while.334
  187.5 3.4 while.334
  193.3 3.4 while.334
  204.8 46.2 %while.329 = (s32[]{:T(128)}, f32[7,512]{1,0:T(8,128)S(1)}, f32[8,2]{1,0:T(8,128)S(1)}, s32[8,7,512]{2,1,0:T(8,128)S(1)}, f32[8,7,512]{2,1,0:T(8,128)S(1)}, /*in...) while((s32[]{:T(128)}, f32[7,512]{1,0:T(8,128)S(1)}, ...), condition=%wide.region_12.12_spmd, body=%wide.region_7.11_spmd.sunk | while | flops 6075146 | bytes 502252 | solution.py:103
  246.0 3.4 while.334
  251.8 46.2 %while.329 = (s32[]{:T(128)}, f32[7,512]{1,0:T(8,128)S(1)}, f32[8,2]{1,0:T(8,128)S(1)}, s32[8,7,512]{2,1,0:T(8,128)S(1)}, f32[8,7,512]{2,1,0:T(8,128)S(1)}, /*in...) while((s32[]{:T(128)}, f32[7,512]{1,0:T(8,128)S(1)}, ...), condition=%wide.region_12.12_spmd, body=%wide.region_7.11_spmd.sunk | while | flops 6075146 | bytes 502252 | solution.py:103
  300.5 162.3 %psum.29 = f32[8]{0:T(128)S(1)} all-reduce(f32[8]{0:T(128)S(1)} %psum.28), channel_id=1, replica_groups=mesh['types'=16,'tm'=2] {'types'}, use_global_device_ids=true, to_apply=%region_16.17 | all-reduce | flops 8 | bytes 64 | tf_op jit(solution)/shard_map/psum | solution.py:200
  465.1 145.1 %while.325 = (s32[]{:T(128)}, f32[3,8,7,512]{3,2,1,0:T(8,128)S(1)}, f32[3,8,7,512]{3,2,1,0:T(8,128)S(1)}, f32[3,8,7,512]{3,2,1,0:T(8,128)S(1)}, f32[3,7,512]{2,1...) while((s32[]{:T(128)}, f32[3,8,7,512]{3,2,1,0:T(8,128)S(1)}, ...), condition=%wide.region_22.23_spmd, body=%wide.region_17.22_spmd.sunk | while | flops 6097422 | bytes 1872697 | solution.py:173
  466.4 47.0 %while.330 = (s32[]{:T(128)}, f32[7,512]{1,0:T(8,128)S(1)}, f32[8,7,512]{2,1,0:T(8,128)S(1)}, f32[8,7,512]{2,1,0:T(8,128)S(1)}, f32[8,7,512]{2,1,0:T(8,128)S(1)}...) while((s32[]{:T(128)}, f32[7,512]{1,0:T(8,128)S(1)}, ...), condition=%wide.region_21.21_spmd.clone.clone, body=%wide.region_18.20_spmd.clone.clone.sunk | while | flops 6097420 | bytes 483244 | solution.py:77
  514.8 47.0 %while.330 = (s32[]{:T(128)}, f32[7,512]{1,0:T(8,128)S(1)}, f32[8,7,512]{2,1,0:T(8,128)S(1)}, f32[8,7,512]{2,1,0:T(8,128)S(1)}, f32[8,7,512]{2,1,0:T(8,128)S(1)}...) while((s32[]{:T(128)}, f32[7,512]{1,0:T(8,128)S(1)}, ...), condition=%wide.region_21.21_spmd.clone.clone, body=%wide.region_18.20_spmd.clone.clone.sunk | while | flops 6097420 | bytes 483244 | solution.py:77
  563.1 47.0 %while.330 = (s32[]{:T(128)}, f32[7,512]{1,0:T(8,128)S(1)}, f32[8,7,512]{2,1,0:T(8,128)S(1)}, f32[8,7,512]{2,1,0:T(8,128)S(1)}, f32[8,7,512]{2,1,0:T(8,128)S(1)}...) while((s32[]{:T(128)}, f32[7,512]{1,0:T(8,128)S(1)}, ...), condition=%wide.region_21.21_spmd.clone.clone, body=%wide.region_18.20_spmd.clone.clone.sunk | while | flops 6097420 | bytes 483244 | solution.py:77
  610.2 140.8 %while.327 = (s32[]{:T(128)}, f32[3,2,8]{2,1,0:T(2,128)S(1)}, f32[3,7,512]{2,1,0:T(8,128)S(1)}, s32[3,8,7,512]{3,2,1,0:T(8,128)S(1)}, f32[3,8,7,512]{3,2,1,0:T(8...) while((s32[]{:T(128)}, f32[3,2,8]{2,1,0:T(2,128)S(1)}, ...), condition=%wide.region_30.31_spmd, body=%wide.region_23.30_spmd.sunk | while | flops 6075148 | bytes 1450953 | solution.py:188
  610.9 46.2 %while.331 = (s32[]{:T(128)}, f32[7,512]{1,0:T(8,128)S(1)}, f32[8,2]{1,0:T(8,128)S(1)}, s32[8,7,512]{2,1,0:T(8,128)S(1)}, f32[8,7,512]{2,1,0:T(8,128)S(1)}, /*in...) while((s32[]{:T(128)}, f32[7,512]{1,0:T(8,128)S(1)}, ...), condition=%wide.region_29.29_spmd, body=%wide.region_24.28_spmd.sunk | while | flops 6075146 | bytes 502252 | solution.py:103
  611.7 3.4 while.332
  657.9 46.2 %while.331 = (s32[]{:T(128)}, f32[7,512]{1,0:T(8,128)S(1)}, f32[8,2]{1,0:T(8,128)S(1)}, s32[8,7,512]{2,1,0:T(8,128)S(1)}, f32[8,7,512]{2,1,0:T(8,128)S(1)}, /*in...) while((s32[]{:T(128)}, f32[7,512]{1,0:T(8,128)S(1)}, ...), condition=%wide.region_29.29_spmd, body=%wide.region_24.28_spmd.sunk | while | flops 6075146 | bytes 502252 | solution.py:103
  681.7 3.4 while.332
  699.0 3.4 while.332
  704.8 46.2 %while.331 = (s32[]{:T(128)}, f32[7,512]{1,0:T(8,128)S(1)}, f32[8,2]{1,0:T(8,128)S(1)}, s32[8,7,512]{2,1,0:T(8,128)S(1)}, f32[8,7,512]{2,1,0:T(8,128)S(1)}, /*in...) while((s32[]{:T(128)}, f32[7,512]{1,0:T(8,128)S(1)}, ...), condition=%wide.region_29.29_spmd, body=%wide.region_24.28_spmd.sunk | while | flops 6075146 | bytes 502252 | solution.py:103
  751.1 165.4 %all_gather.7 = f32[96,2,8]{2,1,0:T(2,128)S(1)} all-gather(f32[3,2,8]{2,1,0:T(2,128)S(1)} %get-tuple-element.1994), channel_id=1, replica_groups=mesh['types'=16,'tm'=2] {'types','tm'}, dimensions={0}, use_global_device_ids=true | all-gather | bytes 6336 | tf_op jit(solution)/shard_map/all_gather | solution.py:203
  916.7 46.2 %all-reduce.2 = f32[96]{0:T(128)S(1)} all-reduce(f32[96]{0:T(128)S(1)} %dynamic-slice_dynamic-update-slice_fusion), channel_id=1, replica_groups=mesh['types'=16,'tm'=2] {'types','tm'}, use_global_device_ids=true, to_apply=%add.2 | all-reduce | flops 96 | bytes 768
  966.9 29.1 %psum.31 = f32[8]{0:T(128)S(1)} all-reduce(f32[8]{0:T(128)S(1)} %psum.30), channel_id=1, replica_groups=mesh['types'=16,'tm'=2] {'types'}, use_global_device_ids=true, to_apply=%region_33.34 | all-reduce | flops 8 | bytes 64 | tf_op jit(solution)/shard_map/psum | solution.py:200
  (2656 shorter events, 652.5 us)
Async XLA Ops:
  0.6 462.1 %copy-start = (f32[8,8]{1,0:T(8,128)S(1)}, f32[8,8]{1,0:T(8,128)}, u32[]{:S(2)}) copy-start(f32[8,8]{1,0:T(8,128)} %param.46) | copy-start | bytes 772
  0.6 10.4 %all-to-all-start = ((s32[6,4,7,512]{3,1,2,0:T(4,128)}), s32[6,4,7,512]{3,1,2,0:T(4,128)S(1)}, u32[]{:S(2)}, u32[]{:S(2)}) async-start(s32[6,4,7,512]{3,1,2,0:T(4,128)} %param.36), calls=%async_computation | async-start | bytes 688128 | tf_op jit(solution)/shard_map/all_to_all | solution.py:133
  4.1 0.7 copy-start.5
  4.8 0.7 copy-start.8
  7.4 0.7 copy-start.4
  8.1 0.7 copy-start.3
  9.5 0.7 copy-start.2
  10.3 0.7 copy-start.7
  11.3 0.7 copy-start.6
  12.0 145.2 %copy-start.1 = (f32[6,7,512]{2,1,0:T(8,128)S(1)}, f32[6,7,512]{2,1,0:T(8,128)}, u32[]{:S(2)}) copy-start(f32[6,7,512]{2,1,0:T(8,128)} %param.38) | copy-start | bytes 258052
  300.5 162.3 %copy-start.10 = (f32[8]{0:T(128)S(1)}, f32[8]{0:T(128)}, u32[]{:S(2)}) copy-start(f32[8]{0:T(128)} %param.44) | copy-start | bytes 100
  965.3 0.7 copy-start.9
  996.0 0.5 copy-start.11
